TPU v7x, 32 devices: a whole 2x2x4 slice. The times are simulated.
32 devices in a mesh: samp: 4 (over z), seq: 8 (over y, x, core).
Axes of the slice: x: 2, y: 2, z: 4, core: 2. Of those that a mesh axis runs over, the one named last changes fastest.
Arguments:
- queries: bfloat16 [4, 4096, 3584], P('samp', 'seq'), may hold values from -200 to 200
- keys: bfloat16 [4, 4096, 512], P('samp', 'seq'), may hold values from -6 to 6
- values: bfloat16 [4, 4096, 512], P('samp', 'seq'), may hold values from -6 to 6
- reg_owner: int32 [4], P('samp'), may hold values from 0 to 7
- block_lists: int32 [4, 32, 8], P('samp', 'seq'), may hold values from 0 to 31, as said below
- list_counts: int32 [4, 32], P('samp', 'seq'), may hold values from 0 to 8, as said below
- image_blocks: int32 [4, 32], P('samp', 'seq'), may hold values from 0 to 1, as said below
Outputs:
- attended: bfloat16 [4, 4096, 3584], P('samp', 'seq')
Inputs may be any that keep to these rules, and one draw needn't show every extreme that they name: `block_lists`: block b lies on sequence index b // 4. Entry t of a list is used only where t < the block's count, unused entries are 0. The used entries of one block name blocks of distinct sequence indices other than its own. Over all blocks of one sequence index, at most one distinct block of each other sequence index is named. On the last sequence index of each sample, the lists together name a block of every other index. `list_counts`: 0 for image blocks; at most 8. `image_blocks`: the blocks of the last sequence index of each sample are text blocks.
All inputs are finite; a program needn't handle non-finite values.
Results may differ from a plain program's by a relative error of at most 0.0043.
Values may be sent and summed in bfloat16 or wider, within the bound.
A program may use at most 128 MiB of HBM per device.

v0:
```python
import math

import jax
import jax.numpy as jnp
from jax import lax
from jax.sharding import PartitionSpec as P

QUERY_HEADS = 28
KEY_VALUE_HEADS = 4
HEAD_SIZE = 128
REG = 64


very_low = -1e30


def broadcast(value, axis, source):
    kept = jnp.where(lax.axis_index(axis) == source, value, 0).astype(value.dtype)
    return lax.psum(kept, axis)


def group_part(query_row_list, key_row_list, value_row_list, visible):
    head_grouped = query_row_list.reshape(
        query_row_list.shape[0], KEY_VALUE_HEADS, QUERY_HEADS // KEY_VALUE_HEADS, HEAD_SIZE
    )
    per_head_keys = key_row_list.reshape(-1, KEY_VALUE_HEADS, HEAD_SIZE)
    per_head_values = value_row_list.reshape(-1, KEY_VALUE_HEADS, HEAD_SIZE)
    scores = jnp.einsum(
        "qhgd,khd->hgqk", head_grouped, per_head_keys, preferred_element_type=jnp.float32
    ) / math.sqrt(HEAD_SIZE)
    scores = jnp.where(visible, scores, very_low)
    maxima = jnp.max(scores, axis=-1)
    weights = jnp.where(visible, jnp.exp(scores - maxima[..., None]), 0.0)
    totals = jnp.sum(weights, axis=-1)
    partial_value = jnp.einsum(
        "hgqk,khd->hgqd",
        weights.astype(jnp.bfloat16),
        per_head_values,
        preferred_element_type=jnp.float32,
    )
    return (maxima, totals, partial_value)


def combine(parts):
    top_score = jnp.maximum(jnp.maximum(parts[0][0], parts[1][0]), parts[2][0])
    numerator = jnp.zeros(parts[0][2].shape, jnp.float32)
    denominator = jnp.zeros(parts[0][1].shape, jnp.float32)
    for maxima, totals, partial_value in parts:
        rescale = jnp.exp(maxima - top_score)
        numerator = numerator + rescale[..., None] * partial_value
        denominator = denominator + rescale * totals
    merged = numerator / denominator[..., None]
    return merged.transpose(2, 0, 1, 3).reshape(merged.shape[2], -1)


def per_device(queries, keys, values, reg_owner, block_lists, list_counts, image_blocks):
    query_all = queries[0]
    every_key = keys[0]
    every_value = values[0]
    local_lists = block_lists[0]
    local_counts = list_counts[0]
    local_image = image_blocks[0]
    devices = lax.axis_size("seq")
    position = lax.axis_index("seq")
    blocks_here = local_lists.shape[0]
    slot_count = local_lists.shape[1]
    rows_block = every_key.shape[0] // blocks_here
    kv_width = every_key.shape[1]
    stacked = jnp.stack([every_key[:REG], every_value[:REG]])
    registers = broadcast(stacked, "seq", reg_owner[0])
    reg_keys = registers[0]
    reg_values = registers[1]
    all_lists, all_counts = (
        lax.all_gather(local_lists, "seq", axis=0, tiled=True),
        lax.all_gather(local_counts, "seq", axis=0, tiled=True),
    )
    own_ids = position * blocks_here + jnp.arange(blocks_here, dtype=jnp.int32)
    live_slots = jnp.arange(slot_count, dtype=jnp.int32)[None, :] < all_counts[:, None]
    named_here = (all_lists[:, :, None] == own_ids[None, None, :]) & live_slots[:, :, None]
    wanted = jnp.any(named_here, axis=1).reshape(devices, blocks_here, blocks_here)
    selector = jnp.any(wanted, axis=1).astype(jnp.bfloat16)
    send_keys = jnp.dot(
        selector,
        every_key.reshape(blocks_here, rows_block * kv_width),
        preferred_element_type=jnp.float32,
    ).astype(jnp.bfloat16)
    send_values = jnp.dot(
        selector,
        every_value.reshape(blocks_here, rows_block * kv_width),
        preferred_element_type=jnp.float32,
    ).astype(jnp.bfloat16)
    owners = (local_lists // blocks_here).reshape(-1)
    got_keys, got_values = (
        lax.all_to_all(
            send_keys.reshape(devices, rows_block, kv_width),
            "seq",
            split_axis=0,
            concat_axis=0,
            tiled=True,
        ),
        lax.all_to_all(
            send_values.reshape(devices, rows_block, kv_width),
            "seq",
            split_axis=0,
            concat_axis=0,
            tiled=True,
        ),
    )
    remote_keys = got_keys[owners]
    remote_values = got_values[owners]
    remote_keys = remote_keys.reshape(blocks_here, slot_count * rows_block, kv_width)
    remote_values = remote_values.reshape(blocks_here, slot_count * rows_block, kv_width)
    row_ids = jnp.arange(rows_block)
    slot_rows = jnp.arange(slot_count * rows_block) // rows_block

    def attend(pieces):
        query_row_list, own_keys, own_values, named_keys, named_values, list_count, is_image = (
            pieces
        )
        reg_visible = jnp.ones((rows_block, reg_keys.shape[0]), bool)
        own_visible = (row_ids[None, :] <= row_ids[:, None]) | (is_image == 1)
        far_visible = jnp.broadcast_to(
            slot_rows[None, :] < list_count, (rows_block, slot_count * rows_block)
        )
        parts = [
            group_part(query_row_list, reg_keys, reg_values, reg_visible),
            group_part(query_row_list, own_keys, own_values, own_visible),
            group_part(query_row_list, named_keys, named_values, far_visible),
        ]
        return combine(parts).astype(jnp.bfloat16)

    blocks_out = lax.map(
        attend,
        (
            query_all.reshape(blocks_here, rows_block, -1),
            every_key.reshape(blocks_here, rows_block, kv_width),
            every_value.reshape(blocks_here, rows_block, kv_width),
            remote_keys,
            remote_values,
            local_counts,
            local_image,
        ),
    )
    return blocks_out.reshape(1, blocks_here * rows_block, -1)


def solution(mesh):
    placed = (
        P("samp", "seq", None),
        P("samp", "seq", None),
        P("samp", "seq", None),
        P("samp"),
        P("samp", "seq", None),
        P("samp", "seq"),
        P("samp", "seq"),
    )
    return jax.shard_map(
        per_device, mesh=mesh, in_specs=placed, out_specs=P("samp", "seq", None), check_vma=False
    )
```

profile of v0, /device:TPU:0, one launch (start us, length us, event | category | flops | bytes accessed | tf_op | source)
XLA Modules:
  0.0 281.8 jit_solution(2486919620880724648)
XLA Ops:
  6.5 1.3 dynamic-slice
  9.2 9.5 %all-reduce = s32[32]{0:T(128)S(1)} all-reduce(s32[32]{0:T(128)S(1)} %bitcast_dynamic-update-slice_fusion), channel_id=3, replica_groups=mesh['samp'=4,'seq'=8] {'seq'}, use_global_device_ids=true, to_apply=%add | all-reduce | flops 32 | bytes 256
  18.8 8.3 %all-gather = s32[1,32,8]{2,0,1:T(1,128)S(1)} all-gather(s32[1,4,8]{2,0,1:T(1,128)} %bitcast.266), channel_id=2, replica_groups=mesh['samp'=4,'seq'=8] {'seq'}, dimensions={1}, use_global_device_ids=true | all-gather | bytes 1152 | tf_op jit(solution)/shard_map/all_gather | solution.py:74
  27.3 1.4 reshape_squeeze.23
  29.4 1.3 copy.75
  30.7 3.6 %all-to-all-start = ((bf16[8,128,512]{2,1,0:T(8,128)(2,1)}), bf16[8,128,512]{2,1,0:T(8,128)(2,1)S(1)}, u32[]{:S(2)}, u32[]{:S(2)}) async-start(bf16[8,128,512]{2,1,0:T(8,128)(2,1)} %copy.75), calls=%async_computation | async-start | bytes 2097152 | tf_op jit(solution)/shard_map/all_to_all | solution.py:94
  36.5 13.1 %all-to-all-done = bf16[8,128,512]{2,1,0:T(8,128)(2,1)S(1)} async-done(((bf16[8,128,512]{2,1,0:T(8,128)(2,1)}), bf16[8,128,512]{2,1,0:T(8,128)(2,1)S(1)}, u32[]{:S(2)}, u32[]{:S(2)}) %all-to-all-start) | async-done | bytes 1048608 | tf_op jit(solution)/shard_map/all_to_all | solution.py:94
  49.6 3.6 %all-to-all-start.1 = ((bf16[8,128,512]{2,1,0:T(8,128)(2,1)}), bf16[8,128,512]{2,1,0:T(8,128)(2,1)S(1)}, u32[]{:S(2)}, u32[]{:S(2)}) async-start(bf16[8,128,512]{2,1,0:T(8,128)(2,1)} %copy.76), calls=%async_computation.1 | async-start | bytes 2097152 | tf_op jit(solution)/shard_map/all_to_all | solution.py:101
  54.8 57.3 %all-reduce.3.cloned.1.call-done = bf16[2,64,512]{2,1,0:T(8,128)(2,1)} async-done(((bf16[2,64,512]{2,1,0:T(8,128)(2,1)}), bf16[2,64,512]{2,1,0:T(8,128)(2,1)}) %all-reduce.3.cloned.1.call-update) | async-done | bytes 131088 | tf_op jit(solution)/shard_map/psum | solution.py:19
  114.4 2.8 gather_fusion
  117.1 2.8 %gather_fusion.1 = bf16[32,128,512]{2,1,0:T(8,128)(2,1)} fusion(bf16[8,128,512]{2,1,0:T(8,128)(2,1)S(1)} %all-to-all-done.1, s32[1024]{0:T(1024)S(1)} %pad_clamp_fusion), kind=kCustom, calls=%fused_computation.1 | custom fusion | bytes 8388736 | tf_op jit(solution)/shard_map/gather | solution.py:110
  120.0 155.0 %while.12 = (s32[]{:T(128)}, bf16[4,128,3584]{2,1,0:T(8,128)(2,1)}, bf16[4,128,3584]{2,1,0:T(8,128)(2,1)}, bf16[1,64,512]{2,1,0:T(8,128)(2,1)}, s32[4]{0:T(128)S...) while((s32[]{:T(128)}, bf16[4,128,3584]{2,1,0:T(8,128)(2,1)}, ...), condition=%wide.wide.region_10.11_spmd.clone, body=%wide.wide.region_3.10_spmd.clone.sunk | while | flops 2289687552 | bytes 161137776 | solution.py:132
  124.2 3.0 %constant_dynamic-slice_fusion.13 = (bf16[1,1024,512]{2,1,0:T(8,128)(2,1)}, bf16[1,1024,512]{2,1,0:T(8,128)(2,1)}) fusion(bf16[4,1024,512]{2,1,0:T(8,128)(2,1)} %get-tuple-element.384, s32[]{:T(128)} %get-tuple-element.359, bf16[4,1024,512]{2,1,0:T(8,128)(2,1)} %get-tuple-element.381), kind=kLoop, calls=%fused_computation.65.clone.clone.1 | loop fusion | bytes 4194308 | tf_op jit(solution)/shard_map/while/body/jit(dynamic_index_in_dim)/dynamic_slice | solution.py:132
  127.2 2.3 copy.137
  130.8 4.4 %bitcast_reduce_fusion.3 = (f32[4,7,128]{2,1,0:T(8,128)S(1)}, f32[4,1024,128,7]{2,1,3,0:T(8,128)S(1)}) fusion(pred[1024]{0:T(1024)(128)(4,1)S(1)} %fusion.129, bf16[1024,4,128,1]{0,2,3,1:T(8,128)(2,1)} %bitcast.250, bf16[128,4,7,128]{0,3,2,1:T(8,128)(2,1)S(1)} %bitcast.248), kind=kOutput, calls=%fused_computation.5.clone.clone.1 | convolution fusion | flops 950530560 | bytes 16661504 | tf_op jit(solution)/shard_map/while/body/eval_jaxpr/qhgd,khd->hgqk/dot_general | solution.py:28
  135.2 4.2 %fusion.130 = f32[4,7,128]{2,1,0:T(8,128)S(1)} fusion(f32[4,1024,128,7]{2,1,3,0:T(8,128)S(1)} %get-tuple-element.338, f32[4,7,128]{2,1,0:T(8,128)S(1)} %get-tuple-element.339, pred[1024]{0:T(1024)(128)(4,1)S(1)} %fusion.129), kind=kLoop, calls=%fused_computation.9.clone.clone.1 | loop fusion | flops 18346496 | bytes 14709760 | tf_op jit(solution)/shard_map/while/body/eval_jaxpr/reduce_sum | solution.py:34
  142.0 1.9 fusion.126
  143.9 1.7 fusion.128
  145.6 1.5 copy.136
  147.1 9.1 %fusion.134 = bf16[128,4,7,128]{0,3,2,1:T(8,128)(2,1)} fusion(f32[4,7,128,128]{2,3,1,0:T(8,128)S(1)} %copy-done.3, f32[4,7,128,128]{2,3,1,0:T(8,128)} %fusion.128, bf16[1024,4,128,1]{0,2,3,1:T(8,128)(2,1)S(1)} %bitcast.251, f32[4,1024,128,7]{2,1,3,0:T(8,128)} %copy-done, f32[4,7,128]{2,1,0:T(8,128)S(1)} %get-tuple-element.339, ...), kind=kOutput, calls=%fused_computation.17.clone.clone.1 | convolution fusion | flops 961085440 | bytes 20388864 | tf_op jit(solution)/shard_map/while/body/eval_jaxpr/hgqk,khd->hgqd/dot_general | solution.py:35
  156.2 1.5 copy.138
  162.9 3.0 %constant_dynamic-slice_fusion.13 = (bf16[1,1024,512]{2,1,0:T(8,128)(2,1)}, bf16[1,1024,512]{2,1,0:T(8,128)(2,1)}) fusion(bf16[4,1024,512]{2,1,0:T(8,128)(2,1)} %get-tuple-element.384, s32[]{:T(128)} %get-tuple-element.359, bf16[4,1024,512]{2,1,0:T(8,128)(2,1)} %get-tuple-element.381), kind=kLoop, calls=%fused_computation.65.clone.clone.1 | loop fusion | bytes 4194308 | tf_op jit(solution)/shard_map/while/body/jit(dynamic_index_in_dim)/dynamic_slice | solution.py:132
  165.9 2.3 copy.137
  169.5 4.4 %bitcast_reduce_fusion.3 = (f32[4,7,128]{2,1,0:T(8,128)S(1)}, f32[4,1024,128,7]{2,1,3,0:T(8,128)S(1)}) fusion(pred[1024]{0:T(1024)(128)(4,1)S(1)} %fusion.129, bf16[1024,4,128,1]{0,2,3,1:T(8,128)(2,1)} %bitcast.250, bf16[128,4,7,128]{0,3,2,1:T(8,128)(2,1)S(1)} %bitcast.248), kind=kOutput, calls=%fused_computation.5.clone.clone.1 | convolution fusion | flops 950530560 | bytes 16661504 | tf_op jit(solution)/shard_map/while/body/eval_jaxpr/qhgd,khd->hgqk/dot_general | solution.py:28
  174.0 4.2 %fusion.130 = f32[4,7,128]{2,1,0:T(8,128)S(1)} fusion(f32[4,1024,128,7]{2,1,3,0:T(8,128)S(1)} %get-tuple-element.338, f32[4,7,128]{2,1,0:T(8,128)S(1)} %get-tuple-element.339, pred[1024]{0:T(1024)(128)(4,1)S(1)} %fusion.129), kind=kLoop, calls=%fused_computation.9.clone.clone.1 | loop fusion | flops 18346496 | bytes 14709760 | tf_op jit(solution)/shard_map/while/body/eval_jaxpr/reduce_sum | solution.py:34
  180.8 1.9 fusion.126
  182.7 1.7 fusion.128
  184.3 1.5 copy.136
  185.8 9.1 %fusion.134 = bf16[128,4,7,128]{0,3,2,1:T(8,128)(2,1)} fusion(f32[4,7,128,128]{2,3,1,0:T(8,128)S(1)} %copy-done.3, f32[4,7,128,128]{2,3,1,0:T(8,128)} %fusion.128, bf16[1024,4,128,1]{0,2,3,1:T(8,128)(2,1)S(1)} %bitcast.251, f32[4,1024,128,7]{2,1,3,0:T(8,128)} %copy-done, f32[4,7,128]{2,1,0:T(8,128)S(1)} %get-tuple-element.339, ...), kind=kOutput, calls=%fused_computation.17.clone.clone.1 | convolution fusion | flops 961085440 | bytes 20388864 | tf_op jit(solution)/shard_map/while/body/eval_jaxpr/hgqk,khd->hgqd/dot_general | solution.py:35
  195.0 1.5 copy.138
  201.7 3.0 %constant_dynamic-slice_fusion.13 = (bf16[1,1024,512]{2,1,0:T(8,128)(2,1)}, bf16[1,1024,512]{2,1,0:T(8,128)(2,1)}) fusion(bf16[4,1024,512]{2,1,0:T(8,128)(2,1)} %get-tuple-element.384, s32[]{:T(128)} %get-tuple-element.359, bf16[4,1024,512]{2,1,0:T(8,128)(2,1)} %get-tuple-element.381), kind=kLoop, calls=%fused_computation.65.clone.clone.1 | loop fusion | bytes 4194308 | tf_op jit(solution)/shard_map/while/body/jit(dynamic_index_in_dim)/dynamic_slice | solution.py:132
  204.7 2.3 copy.137
  208.3 4.4 %bitcast_reduce_fusion.3 = (f32[4,7,128]{2,1,0:T(8,128)S(1)}, f32[4,1024,128,7]{2,1,3,0:T(8,128)S(1)}) fusion(pred[1024]{0:T(1024)(128)(4,1)S(1)} %fusion.129, bf16[1024,4,128,1]{0,2,3,1:T(8,128)(2,1)} %bitcast.250, bf16[128,4,7,128]{0,3,2,1:T(8,128)(2,1)S(1)} %bitcast.248), kind=kOutput, calls=%fused_computation.5.clone.clone.1 | convolution fusion | flops 950530560 | bytes 16661504 | tf_op jit(solution)/shard_map/while/body/eval_jaxpr/qhgd,khd->hgqk/dot_general | solution.py:28
  212.7 4.2 %fusion.130 = f32[4,7,128]{2,1,0:T(8,128)S(1)} fusion(f32[4,1024,128,7]{2,1,3,0:T(8,128)S(1)} %get-tuple-element.338, f32[4,7,128]{2,1,0:T(8,128)S(1)} %get-tuple-element.339, pred[1024]{0:T(1024)(128)(4,1)S(1)} %fusion.129), kind=kLoop, calls=%fused_computation.9.clone.clone.1 | loop fusion | flops 18346496 | bytes 14709760 | tf_op jit(solution)/shard_map/while/body/eval_jaxpr/reduce_sum | solution.py:34
  219.5 1.9 fusion.126
  221.4 1.7 fusion.128
  223.1 1.5 copy.136
  224.6 9.1 %fusion.134 = bf16[128,4,7,128]{0,3,2,1:T(8,128)(2,1)} fusion(f32[4,7,128,128]{2,3,1,0:T(8,128)S(1)} %copy-done.3, f32[4,7,128,128]{2,3,1,0:T(8,128)} %fusion.128, bf16[1024,4,128,1]{0,2,3,1:T(8,128)(2,1)S(1)} %bitcast.251, f32[4,1024,128,7]{2,1,3,0:T(8,128)} %copy-done, f32[4,7,128]{2,1,0:T(8,128)S(1)} %get-tuple-element.339, ...), kind=kOutput, calls=%fused_computation.17.clone.clone.1 | convolution fusion | flops 961085440 | bytes 20388864 | tf_op jit(solution)/shard_map/while/body/eval_jaxpr/hgqk,khd->hgqd/dot_general | solution.py:35
  233.7 1.5 copy.138
  240.4 3.0 %constant_dynamic-slice_fusion.13 = (bf16[1,1024,512]{2,1,0:T(8,128)(2,1)}, bf16[1,1024,512]{2,1,0:T(8,128)(2,1)}) fusion(bf16[4,1024,512]{2,1,0:T(8,128)(2,1)} %get-tuple-element.384, s32[]{:T(128)} %get-tuple-element.359, bf16[4,1024,512]{2,1,0:T(8,128)(2,1)} %get-tuple-element.381), kind=kLoop, calls=%fused_computation.65.clone.clone.1 | loop fusion | bytes 4194308 | tf_op jit(solution)/shard_map/while/body/jit(dynamic_index_in_dim)/dynamic_slice | solution.py:132
  243.4 2.3 copy.137
  247.0 4.4 %bitcast_reduce_fusion.3 = (f32[4,7,128]{2,1,0:T(8,128)S(1)}, f32[4,1024,128,7]{2,1,3,0:T(8,128)S(1)}) fusion(pred[1024]{0:T(1024)(128)(4,1)S(1)} %fusion.129, bf16[1024,4,128,1]{0,2,3,1:T(8,128)(2,1)} %bitcast.250, bf16[128,4,7,128]{0,3,2,1:T(8,128)(2,1)S(1)} %bitcast.248), kind=kOutput, calls=%fused_computation.5.clone.clone.1 | convolution fusion | flops 950530560 | bytes 16661504 | tf_op jit(solution)/shard_map/while/body/eval_jaxpr/qhgd,khd->hgqk/dot_general | solution.py:28
  251.4 4.2 %fusion.130 = f32[4,7,128]{2,1,0:T(8,128)S(1)} fusion(f32[4,1024,128,7]{2,1,3,0:T(8,128)S(1)} %get-tuple-element.338, f32[4,7,128]{2,1,0:T(8,128)S(1)} %get-tuple-element.339, pred[1024]{0:T(1024)(128)(4,1)S(1)} %fusion.129), kind=kLoop, calls=%fused_computation.9.clone.clone.1 | loop fusion | flops 18346496 | bytes 14709760 | tf_op jit(solution)/shard_map/while/body/eval_jaxpr/reduce_sum | solution.py:34
  258.3 1.9 fusion.126
  260.1 1.7 fusion.128
  261.8 1.5 copy.136
  263.3 9.1 %fusion.134 = bf16[128,4,7,128]{0,3,2,1:T(8,128)(2,1)} fusion(f32[4,7,128,128]{2,3,1,0:T(8,128)S(1)} %copy-done.3, f32[4,7,128,128]{2,3,1,0:T(8,128)} %fusion.128, bf16[1024,4,128,1]{0,2,3,1:T(8,128)(2,1)S(1)} %bitcast.251, f32[4,1024,128,7]{2,1,3,0:T(8,128)} %copy-done, f32[4,7,128]{2,1,0:T(8,128)S(1)} %get-tuple-element.339, ...), kind=kOutput, calls=%fused_computation.17.clone.clone.1 | convolution fusion | flops 961085440 | bytes 20388864 | tf_op jit(solution)/shard_map/while/body/eval_jaxpr/hgqk,khd->hgqd/dot_general | solution.py:35
  272.5 1.5 copy.138
  (177 shorter events, 40.6 us)
Async XLA Ops:
  6.5 27.7 %copy-start.4 = (bf16[1,512,512]{2,1,0:T(8,128)(2,1)S(1)}, bf16[1,512,512]{2,1,0:T(8,128)(2,1)}, u32[]{:S(2)}) copy-start(bf16[1,512,512]{2,1,0:T(8,128)(2,1)} %param.11) | copy-start | bytes 1572868
  30.7 18.9 %all-to-all-start = ((bf16[8,128,512]{2,1,0:T(8,128)(2,1)}), bf16[8,128,512]{2,1,0:T(8,128)(2,1)S(1)}, u32[]{:S(2)}, u32[]{:S(2)}) async-start(bf16[8,128,512]{2,1,0:T(8,128)(2,1)} %copy.75), calls=%async_computation | async-start | bytes 2097152 | tf_op jit(solution)/shard_map/all_to_all | solution.py:94
  34.2 19.8 %slice-start = ((bf16[1,512,512]{2,1,0:T(8,128)(2,1)}), bf16[1,64,512]{2,1,0:T(8,128)(2,1)S(1)}, s32[]{:S(2)}) async-start(bf16[1,512,512]{2,1,0:T(8,128)(2,1)} %param.11), calls=%async_computation.3 | async-start | bytes 131072 | tf_op jit(solution)/shard_map/slice | solution.py:69
  34.3 19.7 %slice-start.1 = ((bf16[1,512,512]{2,1,0:T(8,128)(2,1)}), bf16[1,64,512]{2,1,0:T(8,128)(2,1)S(1)}, s32[]{:S(2)}) async-start(bf16[1,512,512]{2,1,0:T(8,128)(2,1)} %param.10), calls=%async_computation.4 | async-start | bytes 131072 | tf_op jit(solution)/shard_map/slice | solution.py:69
  34.3 20.4 %copy-start.11 = (s32[1,4,8]{2,1,0:T(4,128)S(1)}, s32[1,4,8]{2,1,0:T(4,128)}, u32[]{:S(2)}) copy-start(s32[1,4,8]{2,1,0:T(4,128)} %param.13) | copy-start | bytes 388
  49.6 67.6 %all-to-all-start.1 = ((bf16[8,128,512]{2,1,0:T(8,128)(2,1)}), bf16[8,128,512]{2,1,0:T(8,128)(2,1)S(1)}, u32[]{:S(2)}, u32[]{:S(2)}) async-start(bf16[8,128,512]{2,1,0:T(8,128)(2,1)} %copy.76), calls=%async_computation.1 | async-start | bytes 2097152 | tf_op jit(solution)/shard_map/all_to_all | solution.py:101
  53.1 59.0 %all-reduce.3.cloned.1.call-start = ((), (), s32[]{:S(2)}) async-start(), calls=%async_computation.2 | async-start | bytes 262144 | tf_op jit(solution)/shard_map/psum | solution.py:19
  113.0 4.1 %copy-start.9 = (bf16[1,64,512]{2,1,0:T(8,128)(2,1)}, bf16[1,64,512]{2,1,0:T(8,128)(2,1)S(1)}, u32[]{:S(2)}) copy-start(bf16[1,64,512]{2,1,0:T(8,128)(2,1)S(1)} %get-tuple-element.352) | copy-start | bytes 196612
  113.0 4.1 %copy-start.10 = (bf16[1,64,512]{2,1,0:T(8,128)(2,1)}, bf16[1,64,512]{2,1,0:T(8,128)(2,1)S(1)}, u32[]{:S(2)}) copy-start(bf16[1,64,512]{2,1,0:T(8,128)(2,1)S(1)} %get-tuple-element.347) | copy-start | bytes 196612
  117.1 2.9 %copy-start.12 = (s32[1,4]{1,0:T(1,128)S(1)}, s32[1,4]{1,0:T(1,128)}, u32[]{:S(2)}) copy-start(s32[1,4]{1,0:T(1,128)} %param.15) | copy-start | bytes 52
  120.0 3.0 %copy-start.6 = (bf16[4,128,512]{2,1,0:T(8,128)(2,1)S(1)}, bf16[4,128,512]{2,1,0:T(8,128)(2,1)}, u32[]{:S(2)}) copy-start(bf16[4,128,512]{2,1,0:T(8,128)(2,1)} %get-tuple-element.379) | copy-start | bytes 1572868 | tf_op jit(solution)/shard_map/while
  123.7 5.8 %copy-start.14 = (s32[4]{0:T(128)S(1)}, s32[4]{0:T(128)}, u32[]{:S(2)}) copy-start(s32[4]{0:T(128)} %get-tuple-element.380) | copy-start | bytes 52 | tf_op jit(solution)/shard_map/while
  135.2 5.2 %copy-start = (f32[4,1024,128,7]{2,1,3,0:T(8,128)}, f32[4,1024,128,7]{2,1,3,0:T(8,128)S(1)}, u32[]{:S(2)}) copy-start(f32[4,1024,128,7]{2,1,3,0:T(8,128)S(1)} %get-tuple-element.338) | copy-start | bytes 44040196 | tf_op jit(solution)/shard_map/while
  135.2 5.2 %copy-start.8 = (bf16[64,4,128]{2,1,0:T(4,128)(2,1)S(1)}, bf16[64,4,128]{2,1,0:T(4,128)(2,1)}, u32[]{:S(2)}) copy-start(bf16[64,4,128]{2,1,0:T(4,128)(2,1)} %get-tuple-element.385) | copy-start | bytes 196612 | tf_op jit(solution)/shard_map/while
  140.4 3.5 %copy-start.7 = (bf16[64,4,128]{2,1,0:T(4,128)(2,1)S(1)}, bf16[64,4,128]{2,1,0:T(4,128)(2,1)}, u32[]{:S(2)}) copy-start(bf16[64,4,128]{2,1,0:T(4,128)(2,1)} %get-tuple-element.386) | copy-start | bytes 196612 | tf_op jit(solution)/shard_map/while
  140.7 1.0 copy-start.1
  141.9 2.1 copy-start.2
  143.9 3.2 %copy-start.3 = (f32[4,7,128,128]{2,3,1,0:T(8,128)S(1)}, f32[4,7,128,128]{2,3,1,0:T(8,128)}, u32[]{:S(2)}) copy-start(f32[4,7,128,128]{2,3,1,0:T(8,128)} %fusion.126) | copy-start | bytes 5505028 | tf_op jit(solution)/shard_map/while
  156.2 2.5 copy-start.5
  156.2 2.5 copy-start.13
  158.7 3.0 %copy-start.6 = (bf16[4,128,512]{2,1,0:T(8,128)(2,1)S(1)}, bf16[4,128,512]{2,1,0:T(8,128)(2,1)}, u32[]{:S(2)}) copy-start(bf16[4,128,512]{2,1,0:T(8,128)(2,1)} %get-tuple-element.379) | copy-start | bytes 1572868 | tf_op jit(solution)/shard_map/while
  162.4 5.8 %copy-start.14 = (s32[4]{0:T(128)S(1)}, s32[4]{0:T(128)}, u32[]{:S(2)}) copy-start(s32[4]{0:T(128)} %get-tuple-element.380) | copy-start | bytes 52 | tf_op jit(solution)/shard_map/while
  173.9 5.2 %copy-start = (f32[4,1024,128,7]{2,1,3,0:T(8,128)}, f32[4,1024,128,7]{2,1,3,0:T(8,128)S(1)}, u32[]{:S(2)}) copy-start(f32[4,1024,128,7]{2,1,3,0:T(8,128)S(1)} %get-tuple-element.338) | copy-start | bytes 44040196 | tf_op jit(solution)/shard_map/while
  173.9 5.2 %copy-start.8 = (bf16[64,4,128]{2,1,0:T(4,128)(2,1)S(1)}, bf16[64,4,128]{2,1,0:T(4,128)(2,1)}, u32[]{:S(2)}) copy-start(bf16[64,4,128]{2,1,0:T(4,128)(2,1)} %get-tuple-element.385) | copy-start | bytes 196612 | tf_op jit(solution)/shard_map/while
  179.1 3.5 %copy-start.7 = (bf16[64,4,128]{2,1,0:T(4,128)(2,1)S(1)}, bf16[64,4,128]{2,1,0:T(4,128)(2,1)}, u32[]{:S(2)}) copy-start(bf16[64,4,128]{2,1,0:T(4,128)(2,1)} %get-tuple-element.386) | copy-start | bytes 196612 | tf_op jit(solution)/shard_map/while
  179.5 1.0 copy-start.1
  180.6 2.1 copy-start.2
  182.7 3.2 %copy-start.3 = (f32[4,7,128,128]{2,3,1,0:T(8,128)S(1)}, f32[4,7,128,128]{2,3,1,0:T(8,128)}, u32[]{:S(2)}) copy-start(f32[4,7,128,128]{2,3,1,0:T(8,128)} %fusion.126) | copy-start | bytes 5505028 | tf_op jit(solution)/shard_map/while
  195.0 2.5 copy-start.5
  195.0 2.5 copy-start.13
  197.5 3.0 %copy-start.6 = (bf16[4,128,512]{2,1,0:T(8,128)(2,1)S(1)}, bf16[4,128,512]{2,1,0:T(8,128)(2,1)}, u32[]{:S(2)}) copy-start(bf16[4,128,512]{2,1,0:T(8,128)(2,1)} %get-tuple-element.379) | copy-start | bytes 1572868 | tf_op jit(solution)/shard_map/while
  201.2 5.8 %copy-start.14 = (s32[4]{0:T(128)S(1)}, s32[4]{0:T(128)}, u32[]{:S(2)}) copy-start(s32[4]{0:T(128)} %get-tuple-element.380) | copy-start | bytes 52 | tf_op jit(solution)/shard_map/while
  212.7 5.2 %copy-start = (f32[4,1024,128,7]{2,1,3,0:T(8,128)}, f32[4,1024,128,7]{2,1,3,0:T(8,128)S(1)}, u32[]{:S(2)}) copy-start(f32[4,1024,128,7]{2,1,3,0:T(8,128)S(1)} %get-tuple-element.338) | copy-start | bytes 44040196 | tf_op jit(solution)/shard_map/while
  212.7 5.2 %copy-start.8 = (bf16[64,4,128]{2,1,0:T(4,128)(2,1)S(1)}, bf16[64,4,128]{2,1,0:T(4,128)(2,1)}, u32[]{:S(2)}) copy-start(bf16[64,4,128]{2,1,0:T(4,128)(2,1)} %get-tuple-element.385) | copy-start | bytes 196612 | tf_op jit(solution)/shard_map/while
  217.9 3.5 %copy-start.7 = (bf16[64,4,128]{2,1,0:T(4,128)(2,1)S(1)}, bf16[64,4,128]{2,1,0:T(4,128)(2,1)}, u32[]{:S(2)}) copy-start(bf16[64,4,128]{2,1,0:T(4,128)(2,1)} %get-tuple-element.386) | copy-start | bytes 196612 | tf_op jit(solution)/shard_map/while
  219.4 2.1 copy-start.2
  221.4 3.2 %copy-start.3 = (f32[4,7,128,128]{2,3,1,0:T(8,128)S(1)}, f32[4,7,128,128]{2,3,1,0:T(8,128)}, u32[]{:S(2)}) copy-start(f32[4,7,128,128]{2,3,1,0:T(8,128)} %fusion.126) | copy-start | bytes 5505028 | tf_op jit(solution)/shard_map/while
  233.7 2.5 copy-start.5
  233.7 2.5 copy-start.13
  236.2 3.0 %copy-start.6 = (bf16[4,128,512]{2,1,0:T(8,128)(2,1)S(1)}, bf16[4,128,512]{2,1,0:T(8,128)(2,1)}, u32[]{:S(2)}) copy-start(bf16[4,128,512]{2,1,0:T(8,128)(2,1)} %get-tuple-element.379) | copy-start | bytes 1572868 | tf_op jit(solution)/shard_map/while
  239.9 5.8 %copy-start.14 = (s32[4]{0:T(128)S(1)}, s32[4]{0:T(128)}, u32[]{:S(2)}) copy-start(s32[4]{0:T(128)} %get-tuple-element.380) | copy-start | bytes 52 | tf_op jit(solution)/shard_map/while
  251.4 5.2 %copy-start = (f32[4,1024,128,7]{2,1,3,0:T(8,128)}, f32[4,1024,128,7]{2,1,3,0:T(8,128)S(1)}, u32[]{:S(2)}) copy-start(f32[4,1024,128,7]{2,1,3,0:T(8,128)S(1)} %get-tuple-element.338) | copy-start | bytes 44040196 | tf_op jit(solution)/shard_map/while
  251.4 5.2 %copy-start.8 = (bf16[64,4,128]{2,1,0:T(4,128)(2,1)S(1)}, bf16[64,4,128]{2,1,0:T(4,128)(2,1)}, u32[]{:S(2)}) copy-start(bf16[64,4,128]{2,1,0:T(4,128)(2,1)} %get-tuple-element.385) | copy-start | bytes 196612 | tf_op jit(solution)/shard_map/while
  256.6 3.5 %copy-start.7 = (bf16[64,4,128]{2,1,0:T(4,128)(2,1)S(1)}, bf16[64,4,128]{2,1,0:T(4,128)(2,1)}, u32[]{:S(2)}) copy-start(bf16[64,4,128]{2,1,0:T(4,128)(2,1)} %get-tuple-element.386) | copy-start | bytes 196612 | tf_op jit(solution)/shard_map/while
  258.1 2.1 copy-start.2
  260.1 3.2 %copy-start.3 = (f32[4,7,128,128]{2,3,1,0:T(8,128)S(1)}, f32[4,7,128,128]{2,3,1,0:T(8,128)}, u32[]{:S(2)}) copy-start(f32[4,7,128,128]{2,3,1,0:T(8,128)} %fusion.126) | copy-start | bytes 5505028 | tf_op jit(solution)/shard_map/while
  272.5 2.5 copy-start.5
  272.5 2.5 copy-start.13
  (2 other events, 1.9 us)
Sparse Core Ops, SparseCore 0:
  57.0 55.1 all-reduce.2
where the time goes:
time: 283 us; the launch traced here: 282 us
  local copies, waits for them, and re-layouts  72.7 us (26%)
  matrix products  72.5 us (26%)
  waiting for transfers between devices  70.4 us (25%)
  other arithmetic  23.2 us (8%)
  blocking collectives  17.8 us (6%)
  between operations  14.9 us (5%)
  starting transfers between devices  7.34 us (3%)
  loops' own time  2.99 us (1%)
    psum x1, waiting for transfers between devices, broadcast(): return lax.psum(kept, axis)  57.3 us
    dot_general x12, matrix products, group_part(): jnp.einsum('hgqk,khd->hgqd', weights.astype(jnp.bfloat16), per_head_value...  50.8 us
    dynamic_slice x40, local copies, waits for them, and re-layouts, per_device(): lax.map(attend, (query_all.reshape(blocks_here, rows_block, -1), every_ke...  40.5 us
    dot_general x12, matrix products, group_part(): jnp.einsum('qhgd,khd->hgqk', head_grouped, per_head_keys, preferred_eleme...  20.7 us
    reduce_sum x12, other arithmetic, group_part(): totals = jnp.sum(weights, axis=-1)  19.6 us
    all_to_all x1, waiting for transfers between devices, per_device(): lax.all_to_all(send_keys.reshape(devices, rows_block, kv_width), 'seq', s...  13.1 us
    dynamic_update_slice x8, local copies, waits for them, and re-layouts, per_device(): lax.map(attend, (query_all.reshape(blocks_here, rows_block, -1), every_ke...  9.99 us
    unnamed x1, blocking collectives  9.49 us
  transfers between devices with their start and end apart: 3, of which 2 were waited for; matrix products, arithmetic and copies ran while one was open for 3% of the time, Pallas kernels for 0%

commit v1 on v0

v1 whole, which is shorter than its diff:
```python
import functools
import math

import jax
import jax.numpy as jnp
from jax import lax
from jax.experimental import pallas as pl
from jax.experimental.pallas import tpu as pltpu
from jax.sharding import PartitionSpec as P

KEY_VALUE_HEADS = 4
HEAD_SIZE = 128
REG = 64
CHUNKS = 8

hidden = -1e30
score_gain = math.log2(math.e) / math.sqrt(HEAD_SIZE)


def pair_order(devices):
    if devices == 8:
        return [(2, 4), (3, 5), (6, 7)]
    rest = list(range(2, devices))
    return [tuple(rest[i : i + 2]) for i in range(0, len(rest), 2)]


def kernel(
    devices,
    lists_ref,
    counts_ref,
    image_ref,
    owner_ref,
    q_hbm,
    k_hbm,
    v_hbm,
    out_ref,
    q_all,
    k_all,
    v_all,
    need_out,
    need_in,
    chunk_out,
    chunk_in,
    reg_out,
    reg_in,
    x_out,
    x_in,
    acc,
    top,
    bias,
    local_sem,
    q_sem,
    send_need,
    recv_need,
    send_chunk,
    recv_chunk,
    send_reg,
    recv_reg,
    send_x,
    recv_x,
):
    me = lax.axis_index("seq")
    blocks, slots = lists_ref.shape
    rows = k_hbm.shape[1]
    heads = q_hbm.shape[1] // HEAD_SIZE
    group = heads // KEY_VALUE_HEADS
    chunk_rows = 2 * REG // CHUNKS
    peers = range(1, devices)

    def peer(k):
        return me ^ k

    barrier = pltpu.get_barrier_semaphore()
    for k in peers:
        pl.semaphore_signal(barrier, inc=1, device_id={"seq": peer(k)})
    k_copy = pltpu.make_async_copy(k_hbm, k_all, local_sem.at[0])
    v_copy = pltpu.make_async_copy(v_hbm, v_all, local_sem.at[1])
    k_copy.start()
    v_copy.start()

    def q_copy(b):
        span = pl.ds(pl.multiple_of(b * rows, rows), rows)
        return pltpu.make_async_copy(q_hbm.at[span], q_all.at[span], q_sem.at[b])

    for b in range(blocks):
        q_copy(b).start()

    lane = lax.broadcasted_iota(jnp.int32, (8, 128), 1)
    wanted = jnp.zeros((8, 128), jnp.int32)
    for b in range(blocks):
        count = counts_ref[b]
        for t in range(slots):
            entry = lists_ref[b, t]
            source = jnp.where(t < count, lax.div(entry, blocks), -1)
            wanted = jnp.where(lane == source, lax.rem(entry, blocks), wanted)
    need_out[...] = wanted
    k_copy.wait()
    v_copy.wait()
    for c in range(CHUNKS):
        whole = k_all if c < CHUNKS // 2 else v_all
        start = (c % (CHUNKS // 2)) * chunk_rows
        chunk_out[c] = whole[0, start : start + chunk_rows]
    pl.semaphore_wait(barrier, devices - 1)

    def need_copy(k):
        return pltpu.make_async_remote_copy(
            need_out, need_in.at[k], send_need.at[k], recv_need.at[k], device_id={"seq": peer(k)}
        )

    def chunk_copy(k):
        return pltpu.make_async_remote_copy(
            chunk_out.at[lax.rem(peer(k), CHUNKS)],
            chunk_in.at[me],
            send_chunk.at[k],
            recv_chunk.at[k],
            device_id={"seq": peer(k)},
        )

    def reg_copy(k):
        return pltpu.make_async_remote_copy(
            reg_out, reg_in.at[me], send_reg.at[k], recv_reg.at[k], device_id={"seq": peer(k)}
        )

    def x_copy(k, g):
        return pltpu.make_async_remote_copy(
            x_out.at[k, g], x_in.at[k, g], send_x.at[k, g], recv_x.at[k, g], device_id={"seq": peer(k)}
        )

    order = list(reversed(peers))
    for k in order:
        need_copy(k).start()
    for k in order:
        chunk_copy(k).start()
    chunk_in[me] = chunk_out[lax.rem(me, CHUNKS)]

    for b in range(blocks):
        count = counts_ref[b]
        for k in peers:
            source = peer(k)
            seen = jnp.int32(0)
            for t in range(slots):
                entry = lists_ref[b, t]
                hit = jnp.logical_and(lax.div(entry, blocks) == source, t < count)
                seen = jnp.where(hit, 1, seen)
            bias[b, k] = jnp.where(seen == 1, 0.0, hidden)

    pairs = pair_order(devices)
    sends = [(1,)] + pairs

    for k in peers:
        need_copy(k).wait_recv()
    for group_of in sends:
        for k in group_of:
            row = need_in[k]
            pick = jnp.sum(jnp.where(lane[:1] == me, row[:1], 0))
            k_block = k_all[pick]
            v_block = v_all[pick]
            for g in range(KEY_VALUE_HEADS):
                columns = slice(g * HEAD_SIZE, (g + 1) * HEAD_SIZE)
                x_out[k, g, :rows] = k_block[:, columns]
                x_out[k, g, rows:] = v_block[:, columns]
        for g in range(KEY_VALUE_HEADS):
            for k in group_of:
                x_copy(k, g).start()

    for k in peers:
        chunk_copy(k).wait_recv()
    mine = chunk_in[owner_ref[0]]
    reg_out[...] = mine
    reg_in[me] = mine
    for k in order:
        reg_copy(k).start()

    def attend(b, g, keys, values, masks, first, last):
        index = g * blocks + b
        row_span = pl.ds(pl.multiple_of(b * rows, rows), rows)
        ones = jnp.ones(values.shape, values.dtype)
        wide = jnp.concatenate([values, ones], axis=1)
        for h in range(group):
            column = pl.ds(pl.multiple_of((g * group + h) * HEAD_SIZE, HEAD_SIZE), HEAD_SIZE)
            here = pl.ds(h * rows, rows)
            query = q_all[row_span, column]
            scores = lax.dot_general(
                query, keys, (((1,), (1,)), ((), ())), preferred_element_type=jnp.float32
            )
            scores = scores * score_gain + masks
            best = jnp.max(scores, axis=1, keepdims=True)
            if first:
                best = jnp.broadcast_to(best, (rows, 128))
            else:
                before = top[index, here]
                best = jnp.maximum(before, best)
            if scores.shape[1] > 128:
                spread = jnp.concatenate([best] * (scores.shape[1] // 128), axis=1)
            else:
                spread = best
            weights = jnp.exp2(scores - spread).astype(jnp.bfloat16)
            product = jnp.dot(weights, wide, preferred_element_type=jnp.float32)
            if not first:
                scale = jnp.exp2(before - best)
                product = product + acc[index, here] * jnp.concatenate([scale, scale], axis=1)
            if last:
                merged = product[:, :HEAD_SIZE] / product[:, HEAD_SIZE:]
                out_ref[row_span, column] = merged.astype(out_ref.dtype)
            else:
                acc[index, here] = product
                top[index, here] = best

    def own_step(i, carry):
        b = i // KEY_VALUE_HEADS
        g = lax.rem(i, KEY_VALUE_HEADS)

        @pl.when(g == 0)
        def _():
            q_copy(b).wait()

        column = pl.ds(pl.multiple_of(g * HEAD_SIZE, HEAD_SIZE), HEAD_SIZE)
        below = lax.broadcasted_iota(jnp.int32, (rows, rows), 1) <= lax.broadcasted_iota(
            jnp.int32, (rows, rows), 0
        )
        shut = jnp.where(image_ref[b] == 1, 0.0, hidden)
        masks = jnp.where(below, 0.0, shut)
        attend(b, g, k_all[b, :, column], v_all[b, :, column], masks, True, False)
        return carry

    lax.fori_loop(0, blocks * KEY_VALUE_HEADS, own_step, 0)

    for k in peers:
        reg_copy(k).wait_recv()

    side = lax.broadcasted_iota(jnp.int32, (1, 256), 1)
    half = CHUNKS // 2

    def reg_step(i, carry):
        g = i // blocks
        b = lax.rem(i, blocks)

        @pl.when(b == 0)
        def _():
            x_copy(1, g).wait_recv()

        column = pl.ds(pl.multiple_of(g * HEAD_SIZE, HEAD_SIZE), HEAD_SIZE)
        fill = jnp.zeros((REG, HEAD_SIZE), jnp.bfloat16)
        reg_keys = reg_in[pl.ds(0, half), :, column].reshape(REG, HEAD_SIZE)
        reg_values = reg_in[pl.ds(half, half), :, column].reshape(REG, HEAD_SIZE)
        keys = jnp.concatenate([x_in[1, g, :rows], reg_keys, fill], axis=0)
        values = jnp.concatenate([x_in[1, g, rows:], reg_values, fill], axis=0)
        masks = jnp.where(side < rows, bias[b, 1], jnp.where(side < rows + REG, 0.0, hidden))
        attend(b, g, keys, values, masks, False, False)
        return carry

    lax.fori_loop(0, blocks * KEY_VALUE_HEADS, reg_step, 0)

    for pair in pairs:

        def far_step(i, carry, pair=pair):
            g = i // blocks
            b = lax.rem(i, blocks)

            @pl.when(b == 0)
            def _():
                for k in pair:
                    x_copy(k, g).wait_recv()

            keys = jnp.concatenate([x_in[k, g, :rows] for k in pair], axis=0)
            values = jnp.concatenate([x_in[k, g, rows:] for k in pair], axis=0)
            masks = jnp.where(side < rows, bias[b, pair[0]], bias[b, pair[-1]])
            attend(b, g, keys, values, masks, False, pair == pairs[-1])
            return carry

        lax.fori_loop(0, blocks * KEY_VALUE_HEADS, far_step, 0)

    for k in peers:
        need_copy(k).wait_send()
        chunk_copy(k).wait_send()
        reg_copy(k).wait_send()
        for g in range(KEY_VALUE_HEADS):
            x_copy(k, g).wait_send()


def per_device(queries, keys, values, reg_owner, block_lists, list_counts, image_blocks):
    devices = lax.axis_size("seq")
    tokens, width = queries.shape[1:]
    kv_width = keys.shape[2]
    blocks = block_lists.shape[1]
    rows = tokens // blocks
    chunk_rows = 2 * REG // CHUNKS
    group_rows = width // kv_width * rows
    bf = jnp.bfloat16
    dma = pltpu.SemaphoreType.DMA
    smem = pl.BlockSpec(memory_space=pltpu.SMEM)
    anywhere = pl.BlockSpec(memory_space=pl.ANY)
    out = pl.pallas_call(
        functools.partial(kernel, devices),
        out_shape=jax.ShapeDtypeStruct((tokens, width), bf),
        in_specs=[smem] * 4 + [anywhere] * 3,
        out_specs=pl.BlockSpec(memory_space=pltpu.VMEM),
        scratch_shapes=[
            pltpu.VMEM((tokens, width), bf),
            pltpu.VMEM((blocks, rows, kv_width), bf),
            pltpu.VMEM((blocks, rows, kv_width), bf),
            pltpu.VMEM((8, 128), jnp.int32),
            pltpu.VMEM((devices, 8, 128), jnp.int32),
            pltpu.VMEM((CHUNKS, chunk_rows, kv_width), bf),
            pltpu.VMEM((devices, chunk_rows, kv_width), bf),
            pltpu.VMEM((chunk_rows, kv_width), bf),
            pltpu.VMEM((devices, chunk_rows, kv_width), bf),
            pltpu.VMEM((devices, KEY_VALUE_HEADS, 2 * rows, HEAD_SIZE), bf),
            pltpu.VMEM((devices, KEY_VALUE_HEADS, 2 * rows, HEAD_SIZE), bf),
            pltpu.VMEM((blocks * KEY_VALUE_HEADS, group_rows, 2 * HEAD_SIZE), jnp.float32),
            pltpu.VMEM((blocks * KEY_VALUE_HEADS, group_rows, 128), jnp.float32),
            pltpu.SMEM((blocks, devices), jnp.float32),
            dma((2,)),
            dma((blocks,)),
            dma((devices,)),
            dma((devices,)),
            dma((devices,)),
            dma((devices,)),
            dma((devices,)),
            dma((devices,)),
            dma((devices, KEY_VALUE_HEADS)),
            dma((devices, KEY_VALUE_HEADS)),
        ],
        compiler_params=pltpu.CompilerParams(
            collective_id=0, has_side_effects=True, vmem_limit_bytes=56 * 1024 * 1024
        ),
    )(
        block_lists[0],
        list_counts[0],
        image_blocks[0],
        reg_owner,
        queries[0],
        keys.reshape(blocks, rows, kv_width),
        values.reshape(blocks, rows, kv_width),
    )
    return out[None]


def solution(mesh):
    placed = (
        P("samp", "seq", None),
        P("samp", "seq", None),
        P("samp", "seq", None),
        P("samp"),
        P("samp", "seq", None),
        P("samp", "seq"),
        P("samp", "seq"),
    )
    return jax.shard_map(
        per_device, mesh=mesh, in_specs=placed, out_specs=P("samp", "seq", None), check_vma=False
    )
```

time: 283 us -> 107 us (0.38)
  Pallas kernels: 0 us -> 102 us
  matrix products: 72.5 us -> 0 us
  waiting for transfers between devices: 70.4 us -> 0 us
  local copies, waits for them, and re-layouts: 72.7 us -> 4.11 us
  other arithmetic: 23.2 us -> 0 us
  blocking collectives: 17.8 us -> 0 us
  between operations: 14.9 us -> 0.66 us
  starting transfers between devices: 7.34 us -> 0 us
  loops' own time: 2.99 us -> 0 us
    pallas_call x0 -> x1, Pallas kernels: none -> 102 us  [per_device(): pl.pallas_call(functools.partial(kernel, devices), out_shape=jax.ShapeDty...]
    dot_general x26 -> x0, matrix products: 72.5 us -> none  [the longest x12 50.8 us: group_part(): jnp.einsum('hgqk,khd->hgqd', weights.astype(jnp.bfloat16), per_head_value...]
    psum x1 -> x0, waiting for transfers between devices: 57.3 us -> none  [broadcast(): return lax.psum(kept, axis)]
    dynamic_slice x40 -> x0, local copies, waits for them, and re-layouts: 40.5 us -> none  [per_device(): lax.map(attend, (query_all.reshape(blocks_here, rows_block, -1), every_ke...]
    reduce_sum x12 -> x0, other arithmetic: 19.6 us -> none  [group_part(): totals = jnp.sum(weights, axis=-1)]
    all_to_all x2 -> x0, waiting for transfers between devices: 13.1 us -> none  [the longest x1 13.1 us: per_device(): lax.all_to_all(send_keys.reshape(devices, rows_block, kv_width), 'seq', s...]
    dynamic_update_slice x8 -> x0, local copies, waits for them, and re-layouts: 9.99 us -> none  [per_device(): lax.map(attend, (query_all.reshape(blocks_here, rows_block, -1), every_ke...]
    unnamed x1 -> x0, blocking collectives: 9.49 us -> none
  transfers between devices with their start and end apart: 3 -> 0, of which waited for: 2 -> 0; matrix products, arithmetic and copies ran while one was open for 3% -> 0% of each run, Pallas kernels for 0% -> 0%
where the time goes in v1:
time: 107 us
  Pallas kernels  102 us (95%)
  local copies, waits for them, and re-layouts  4.11 us (4%)
    pallas_call x1, Pallas kernels, per_device(): pl.pallas_call(functools.partial(kernel, devices), out_shape=jax.ShapeDty...  102 us
    unnamed x1, local copies, waits for them, and re-layouts  4.11 us

profile of v1, /device:TPU:0, one launch (start us, length us, event | category | flops | bytes accessed | tf_op | source)
XLA Modules:
  0.0 106.8 jit_solution(12530601813611165595)
XLA Ops:
  0.7 102.0 %shard_map.73 = bf16[512,3584]{1,0:T(8,128)(2,1)} custom-call(s32[4,8]{1,0:T(4,128)} %bitcast.11, s32[4]{0:T(128)} %bitcast.12, s32[4]{0:T(128)} %bitcast.13, s32[1]{0:T(128)S(6)} %copy.9.owner_ref, bf16[512,3584]{1,0:T(8,128)(2,1)} %bitcast.8, bf16[4,128,512]{2,1,0:T(8,128)(2,1)} %bitcast.9, bf16[4,128,512]{2,1,0:T(8,128)(2,1)} %bitcast.10), custom_call_target="tpu_custom_call" | custom-call | tf_op jit(solution)/shard_map/pallas_call | solution.py:293
  102.6 4.1 %copy.10 = bf16[1,512,3584]{2,1,0:T(8,128)(2,1)} copy(bf16[1,512,3584]{2,1,0:T(8,128)(2,1)} %bitcast.7) | data formatting | bytes 7340032

commit v2 on v1

--- a/solution.py
+++ b/solution.py
@@ -17,11 +17,11 @@
 score_gain = math.log2(math.e) / math.sqrt(HEAD_SIZE)
 
 
-def pair_order(devices):
+def stage_list(devices):
     if devices == 8:
-        return [(2, 4), (3, 5), (6, 7)]
-    rest = list(range(2, devices))
-    return [tuple(rest[i : i + 2]) for i in range(0, len(rest), 2)]
+        return [(1, 2, 4, 3, 5, 6, 7)]
+    rest = list(range(1, devices))
+    return [tuple(rest[i : i + 7]) for i in range(0, len(rest), 7)]
 
 
 def kernel(
@@ -133,23 +133,18 @@
         chunk_copy(k).start()
     chunk_in[me] = chunk_out[lax.rem(me, CHUNKS)]
 
-    for b in range(blocks):
-        count = counts_ref[b]
-        for k in peers:
-            source = peer(k)
-            seen = jnp.int32(0)
-            for t in range(slots):
-                entry = lists_ref[b, t]
-                hit = jnp.logical_and(lax.div(entry, blocks) == source, t < count)
-                seen = jnp.where(hit, 1, seen)
-            bias[b, k] = jnp.where(seen == 1, 0.0, hidden)
-
-    pairs = pair_order(devices)
-    sends = [(1,)] + pairs
-
+    stages = stage_list(devices)
+
+    for k in peers:
+        chunk_copy(k).wait_recv()
+    mine = chunk_in[owner_ref[0]]
+    reg_out[...] = mine
+    reg_in[me] = mine
+    for k in order:
+        reg_copy(k).start()
     for k in peers:
         need_copy(k).wait_recv()
-    for group_of in sends:
+    for group_of in stages:
         for k in group_of:
             row = need_in[k]
             pick = jnp.sum(jnp.where(lane[:1] == me, row[:1], 0))
@@ -163,37 +158,51 @@
             for k in group_of:
                 x_copy(k, g).start()
 
-    for k in peers:
-        chunk_copy(k).wait_recv()
-    mine = chunk_in[owner_ref[0]]
-    reg_out[...] = mine
-    reg_in[me] = mine
-    for k in order:
-        reg_copy(k).start()
+    for b in range(blocks):
+        count = counts_ref[b]
+        for k in peers:
+            source = peer(k)
+            seen = jnp.int32(0)
+            for t in range(slots):
+                entry = lists_ref[b, t]
+                hit = jnp.logical_and(lax.div(entry, blocks) == source, t < count)
+                seen = jnp.where(hit, 1, seen)
+            bias[b, k] = jnp.where(seen == 1, 0.0, hidden)
 
     def attend(b, g, keys, values, masks, first, last):
         index = g * blocks + b
         row_span = pl.ds(pl.multiple_of(b * rows, rows), rows)
         ones = jnp.ones(values.shape, values.dtype)
         wide = jnp.concatenate([values, ones], axis=1)
-        for h in range(group):
-            column = pl.ds(pl.multiple_of((g * group + h) * HEAD_SIZE, HEAD_SIZE), HEAD_SIZE)
-            here = pl.ds(h * rows, rows)
-            query = q_all[row_span, column]
-            scores = lax.dot_general(
+        columns = [
+            pl.ds(pl.multiple_of((g * group + h) * HEAD_SIZE, HEAD_SIZE), HEAD_SIZE)
+            for h in range(group)
+        ]
+        copies = masks.shape[0] // rows
+        repeat = keys.shape[0] // 128
+
+        def scored(part):
+            query = jnp.concatenate([q_all[row_span, columns[h]] for h in part], axis=0)
+            return lax.dot_general(
                 query, keys, (((1,), (1,)), ((), ())), preferred_element_type=jnp.float32
             )
-            scores = scores * score_gain + masks
+
+        parts = [list(range(group))[i : i + 4] for i in range(0, group, 4)]
+        ahead = [scored(part) for part in parts[:1]]
+        for step, part in enumerate(parts):
+            if step + 1 < len(parts):
+                ahead.append(scored(parts[step + 1]))
+            scores = ahead[step]
+            here = pl.ds(part[0] * rows, len(part) * rows)
+            tall = jnp.concatenate([masks] * len(part), axis=0) if copies else masks
+            scores = scores * score_gain + tall
             best = jnp.max(scores, axis=1, keepdims=True)
             if first:
-                best = jnp.broadcast_to(best, (rows, 128))
+                best = jnp.broadcast_to(best, (len(part) * rows, 128))
             else:
                 before = top[index, here]
                 best = jnp.maximum(before, best)
-            if scores.shape[1] > 128:
-                spread = jnp.concatenate([best] * (scores.shape[1] // 128), axis=1)
-            else:
-                spread = best
+            spread = jnp.concatenate([best] * repeat, axis=1) if repeat > 1 else best
             weights = jnp.exp2(scores - spread).astype(jnp.bfloat16)
             product = jnp.dot(weights, wide, preferred_element_type=jnp.float32)
             if not first:
@@ -201,7 +210,9 @@
                 product = product + acc[index, here] * jnp.concatenate([scale, scale], axis=1)
             if last:
                 merged = product[:, :HEAD_SIZE] / product[:, HEAD_SIZE:]
-                out_ref[row_span, column] = merged.astype(out_ref.dtype)
+                merged = merged.astype(out_ref.dtype)
+                for n, h in enumerate(part):
+                    out_ref[row_span, columns[h]] = merged[n * rows : (n + 1) * rows]
             else:
                 acc[index, here] = product
                 top[index, here] = best
@@ -228,47 +239,37 @@
     for k in peers:
         reg_copy(k).wait_recv()
 
-    side = lax.broadcasted_iota(jnp.int32, (1, 256), 1)
     half = CHUNKS // 2
 
-    def reg_step(i, carry):
+    def far_step(i, carry, stage):
         g = i // blocks
         b = lax.rem(i, blocks)
 
         @pl.when(b == 0)
         def _():
-            x_copy(1, g).wait_recv()
-
-        column = pl.ds(pl.multiple_of(g * HEAD_SIZE, HEAD_SIZE), HEAD_SIZE)
-        fill = jnp.zeros((REG, HEAD_SIZE), jnp.bfloat16)
-        reg_keys = reg_in[pl.ds(0, half), :, column].reshape(REG, HEAD_SIZE)
-        reg_values = reg_in[pl.ds(half, half), :, column].reshape(REG, HEAD_SIZE)
-        keys = jnp.concatenate([x_in[1, g, :rows], reg_keys, fill], axis=0)
-        values = jnp.concatenate([x_in[1, g, rows:], reg_values, fill], axis=0)
-        masks = jnp.where(side < rows, bias[b, 1], jnp.where(side < rows + REG, 0.0, hidden))
-        attend(b, g, keys, values, masks, False, False)
+            for k in stage:
+                x_copy(k, g).wait_recv()
+
+        keys = [x_in[k, g, :rows] for k in stage]
+        values = [x_in[k, g, rows:] for k in stage]
+        masks = [jnp.full((1, rows), bias[b, k]) for k in stage]
+        if stage == stages[0]:
+            column = pl.ds(pl.multiple_of(g * HEAD_SIZE, HEAD_SIZE), HEAD_SIZE)
+            fill = jnp.zeros((128 - REG, HEAD_SIZE), jnp.bfloat16)
+            keys += [reg_in[pl.ds(0, half), :, column].reshape(REG, HEAD_SIZE), fill]
+            values += [reg_in[pl.ds(half, half), :, column].reshape(REG, HEAD_SIZE), fill]
+            side = lax.broadcasted_iota(jnp.int32, (1, 128), 1)
+            masks += [jnp.where(side < REG, 0.0, hidden)]
+        keys = jnp.concatenate(keys, axis=0)
+        values = jnp.concatenate(values, axis=0)
+        masks = jnp.concatenate(masks, axis=1)
+        attend(b, g, keys, values, masks, False, stage == stages[-1])
         return carry
 
-    lax.fori_loop(0, blocks * KEY_VALUE_HEADS, reg_step, 0)
-
-    for pair in pairs:
-
-        def far_step(i, carry, pair=pair):
-            g = i // blocks
-            b = lax.rem(i, blocks)
-
-            @pl.when(b == 0)
-            def _():
-                for k in pair:
-                    x_copy(k, g).wait_recv()
-
-            keys = jnp.concatenate([x_in[k, g, :rows] for k in pair], axis=0)
-            values = jnp.concatenate([x_in[k, g, rows:] for k in pair], axis=0)
-            masks = jnp.where(side < rows, bias[b, pair[0]], bias[b, pair[-1]])
-            attend(b, g, keys, values, masks, False, pair == pairs[-1])
-            return carry
-
-        lax.fori_loop(0, blocks * KEY_VALUE_HEADS, far_step, 0)
+    for stage in stages:
+        lax.fori_loop(
+            0, blocks * KEY_VALUE_HEADS, functools.partial(far_step, stage=stage), 0
+        )
 
     for k in peers:
         need_copy(k).wait_send()
@@ -322,7 +323,7 @@
             dma((devices, KEY_VALUE_HEADS)),
         ],
         compiler_params=pltpu.CompilerParams(
-            collective_id=0, has_side_effects=True, vmem_limit_bytes=56 * 1024 * 1024
+            collective_id=0, has_side_effects=True, vmem_limit_bytes=38 * 1024 * 1024 + devices * kv_width * rows * 8
         ),
     )(
         block_lists[0],

time: 107 us -> 50.8 us (0.47)
  Pallas kernels: 102 us -> 41.2 us
  local copies, waits for them, and re-layouts: 4.11 us -> 7.94 us
    pallas_call x1, Pallas kernels: 102 us -> 41.2 us  [per_device(): pl.pallas_call(functools.partial(kernel, devices), out_shape=jax.ShapeDty...]
    unnamed x1 -> x13, local copies, waits for them, and re-layouts: 4.11 us -> 7.94 us
where the time goes in v2:
time: 50.8 us; the launch traced here: 49.8 us
  Pallas kernels  41.2 us (81%)
  local copies, waits for them, and re-layouts  7.94 us (16%)
  between operations  0.67 us (1%)
    pallas_call x1, Pallas kernels, per_device(): pl.pallas_call(functools.partial(kernel, devices), out_shape=jax.ShapeDty...  41.2 us
    unnamed x13, local copies, waits for them, and re-layouts  7.94 us

profile of v2, /device:TPU:0, one launch (start us, length us, event | category | flops | bytes accessed | tf_op | source)
XLA Modules:
  0.0 49.8 jit_solution(3642841241723412777)
XLA Ops:
  0.7 0.0 copy-start
  0.7 2.0 %copy-done = bf16[1,512,3584]{2,1,0:T(8,128)(2,1)S(1)} copy-done((bf16[1,512,3584]{2,1,0:T(8,128)(2,1)S(1)}, bf16[1,512,3584]{2,1,0:T(8,128)(2,1)}, u32[]{:S(2)}) %copy-start) | copy-done | bytes 3670040
  2.7 0.0 copy-start.1
  2.7 1.0 %copy-done.1 = bf16[1,512,512]{2,1,0:T(8,128)(2,1)S(1)} copy-done((bf16[1,512,512]{2,1,0:T(8,128)(2,1)S(1)}, bf16[1,512,512]{2,1,0:T(8,128)(2,1)}, u32[]{:S(2)}) %copy-start.1) | copy-done | bytes 524312
  3.7 0.0 copy-start.2
  3.7 1.0 %copy-done.2 = bf16[1,512,512]{2,1,0:T(8,128)(2,1)S(1)} copy-done((bf16[1,512,512]{2,1,0:T(8,128)(2,1)S(1)}, bf16[1,512,512]{2,1,0:T(8,128)(2,1)}, u32[]{:S(2)}) %copy-start.2) | copy-done | bytes 524312
  4.8 0.0 copy-start.3
  4.8 0.7 %copy-done.3 = s32[1,4,8]{2,1,0:T(4,128)S(1)} copy-done((s32[1,4,8]{2,1,0:T(4,128)S(1)}, s32[1,4,8]{2,1,0:T(4,128)}, u32[]{:S(2)}) %copy-start.3) | copy-done | bytes 152
  5.5 0.0 copy-start.4
  5.5 0.7 %copy-done.4 = s32[1,4]{1,0:T(1,128)S(1)} copy-done((s32[1,4]{1,0:T(1,128)S(1)}, s32[1,4]{1,0:T(1,128)}, u32[]{:S(2)}) %copy-start.4) | copy-done | bytes 40
  6.1 0.0 copy-start.5
  6.1 0.7 %copy-done.5 = s32[1,4]{1,0:T(1,128)S(1)} copy-done((s32[1,4]{1,0:T(1,128)S(1)}, s32[1,4]{1,0:T(1,128)}, u32[]{:S(2)}) %copy-start.5) | copy-done | bytes 40
  6.8 41.2 %shard_map.73 = bf16[512,3584]{1,0:T(8,128)(2,1)S(1)} custom-call(s32[4,8]{1,0:T(4,128)S(1)} %bitcast.11, s32[4]{0:T(128)S(1)} %bitcast.12, s32[4]{0:T(128)S(1)} %bitcast.13, s32[1]{0:T(128)S(6)} %copy.9.owner_ref, bf16[512,3584]{1,0:T(8,128)(2,1)S(1)} %bitcast.8, bf16[4,128,512]{2,1,0:T(8,128)(2,1)S(1)} %bitcast.9, bf16[4,128,512]{2,1,0:T(8,128)(2,1)S(1)} %bitcast.10), custom_call_target="tpu_custom_call" | custom-call | tf_op jit(solution)/shard_map/pallas_call | solution.py:294
  47.9 1.8 %copy.10 = bf16[1,512,3584]{2,1,0:T(8,128)(2,1)} copy(bf16[1,512,3584]{2,1,0:T(8,128)(2,1)S(1)} %bitcast.7) | data formatting | bytes 7340032
Async XLA Ops:
  0.7 2.0 %copy-start = (bf16[1,512,3584]{2,1,0:T(8,128)(2,1)S(1)}, bf16[1,512,3584]{2,1,0:T(8,128)(2,1)}, u32[]{:S(2)}) copy-start(bf16[1,512,3584]{2,1,0:T(8,128)(2,1)} %param.7) | copy-start | bytes 11010052
  2.7 1.0 %copy-start.1 = (bf16[1,512,512]{2,1,0:T(8,128)(2,1)S(1)}, bf16[1,512,512]{2,1,0:T(8,128)(2,1)}, u32[]{:S(2)}) copy-start(bf16[1,512,512]{2,1,0:T(8,128)(2,1)} %param.8) | copy-start | bytes 1572868
  3.7 1.0 %copy-start.2 = (bf16[1,512,512]{2,1,0:T(8,128)(2,1)S(1)}, bf16[1,512,512]{2,1,0:T(8,128)(2,1)}, u32[]{:S(2)}) copy-start(bf16[1,512,512]{2,1,0:T(8,128)(2,1)} %param.9) | copy-start | bytes 1572868
  4.8 0.7 %copy-start.3 = (s32[1,4,8]{2,1,0:T(4,128)S(1)}, s32[1,4,8]{2,1,0:T(4,128)}, u32[]{:S(2)}) copy-start(s32[1,4,8]{2,1,0:T(4,128)} %param.11) | copy-start | bytes 388
  5.5 0.7 %copy-start.4 = (s32[1,4]{1,0:T(1,128)S(1)}, s32[1,4]{1,0:T(1,128)}, u32[]{:S(2)}) copy-start(s32[1,4]{1,0:T(1,128)} %param.12) | copy-start | bytes 52
  6.1 0.7 %copy-start.5 = (s32[1,4]{1,0:T(1,128)S(1)}, s32[1,4]{1,0:T(1,128)}, u32[]{:S(2)}) copy-start(s32[1,4]{1,0:T(1,128)} %param.13) | copy-start | bytes 52
